TPU v7x, 32 devices: a whole 2x2x4 slice. The times are simulated.
32 devices in a mesh: genes: 16 (over z, y, core), cols: 2 (over x).
Axes of the slice: x: 2, y: 2, z: 4, core: 2. Of those that a mesh axis runs over, the one named last changes fastest.
Arguments:
- expression: float32 [384, 40960], P(None, ('genes', 'cols')), may hold values from -200 to 200
- resample: int32 [384], replicated, may hold values from 0 to 383
- labels: int32 [40960, 300], P(('genes', 'cols')), may hold values from 0 to 1, as said below
- ref_kim: float32 [40960], P(('genes', 'cols')), may hold values from 0 to 1
Outputs:
- connectivity: float32 [40960, 300], P(('genes', 'cols'))
- preservation: float32 [2, 300], replicated
Inputs may be any that keep to these rules, and one draw needn't show every extreme that they name: `labels`: each row holds exactly one 1; every module has 32 or more genes.
All inputs are finite; a program needn't handle non-finite values.
Results may differ from a plain program's by a relative error of at most 0.0031.
Values may be sent and summed in bfloat16 or wider, within the bound.
A program may use at most 128 MiB of HBM per device.

v0:
```python
import math
import jax
import jax.numpy as jnp
from jax import lax
from jax.sharding import PartitionSpec as P

G = 40960


def standardize(expression, resample):
    boot = jnp.take(expression, resample, axis=0)
    centered = boot - jnp.mean(boot, axis=0, keepdims=True)
    total = jnp.sum(centered * centered, axis=0, keepdims=True)
    return (centered * lax.rsqrt(total + 1e-06)).astype(jnp.bfloat16)


def local_sums(connectivity, labels, ref_kim):
    member = labels.astype(jnp.float32)
    kim = jnp.sum(connectivity * member, axis=1)
    rowsum = jnp.sum(connectivity, axis=1)
    stacked = jnp.stack(
        [kim, kim * kim, ref_kim, ref_kim * ref_kim, kim * ref_kim, rowsum, jnp.ones_like(kim)],
        axis=1,
    )
    return jnp.dot(
        member.T, stacked, precision=lax.Precision.HIGHEST, preferred_element_type=jnp.float32
    )


def preserve(sums, total_genes):
    counts = sums[:, 6]
    mean_x = sums[:, 0] / (counts * counts)
    var_x = jnp.maximum(sums[:, 1] / (counts * counts * counts) - mean_x * mean_x, 0.0001)
    mean_y = sums[:, 2] / counts
    var_y = jnp.maximum(sums[:, 3] / counts - mean_y * mean_y, 0.01)
    cross = sums[:, 4] / (counts * counts) - mean_x * mean_y
    between = (sums[:, 5] - sums[:, 0]) / (counts * (total_genes - counts))
    density = (mean_x - between) * jnp.sqrt(counts / var_x)
    linked = cross * jnp.sqrt(counts / (var_x * var_y))
    return jnp.stack([density, linked], axis=0)


def tile_term(row_block, column_block, column_ids, module_count):
    scores = lax.dot_general(
        row_block, column_block, (((0,), (0,)), ((), ())), preferred_element_type=jnp.float32
    )
    squares = scores * scores
    adjacency = (squares * squares * squares).astype(jnp.bfloat16)
    member_block = (
        column_ids[:, None] == jnp.arange(module_count, dtype=jnp.int32)[None, :]
    ).astype(jnp.bfloat16)
    return jnp.dot(adjacency, member_block, preferred_element_type=jnp.float32)


def add_tiles(carried, row_block, piece, every_ids, shard_width, module_count):
    span_width = piece.shape[1]
    column_step = shard_width * math.gcd(span_width // shard_width, 8)
    steps_total = span_width // column_step

    def one_step(step_index, accumulated):
        columns = lax.dynamic_slice_in_dim(piece, step_index * column_step, column_step, 1)
        column_ids = lax.dynamic_slice_in_dim(every_ids, step_index * column_step, column_step, 0)
        return accumulated + tile_term(row_block, columns, column_ids, module_count)

    return lax.fori_loop(0, steps_total, one_step, carried)


def local(expression, resample, labels, ref_kim):
    scaled = standardize(expression, resample)
    module_count = labels.shape[1]
    shard_width = scaled.shape[1]
    module_ids = jnp.sum(labels * jnp.arange(module_count, dtype=jnp.int32)[None, :], axis=1)
    row_block = lax.all_gather(scaled, "cols", axis=1, tiled=True)
    panel_ids = lax.all_gather(module_ids, "genes", axis=0, tiled=True)
    initial = jnp.zeros((row_block.shape[1], module_count), jnp.float32)
    partial_value = add_tiles(
        initial,
        row_block,
        lax.all_gather(scaled, "genes", axis=1, tiled=True),
        panel_ids,
        shard_width,
        module_count,
    )
    connectivity = lax.psum_scatter(partial_value, "cols", scatter_dimension=0, tiled=True)
    sums = lax.psum(local_sums(connectivity, labels, ref_kim), ("genes", "cols"))
    return (connectivity, preserve(sums, G))


def solution(mesh):
    placed = (P(None, ("genes", "cols")), P(), P(("genes", "cols"), None), P(("genes", "cols")))
    return jax.shard_map(
        local,
        mesh=mesh,
        in_specs=placed,
        out_specs=(P(("genes", "cols"), None), P()),
        check_vma=False,
    )
```

profile of v0, /device:TPU:0, one launch (start us, length us, event | category | flops | bytes accessed | tf_op | source)
XLA Modules:
  0.0 391.7 jit_solution(1327400909456358095)
XLA Ops:
  7.2 0.0 all-gather.6.cloned.1.call-start
  7.2 0.8 compare_select_fusion
  8.0 0.7 compare_and_fusion
  8.8 2.7 gather_fusion
  11.5 1.9 select_reduce_fusion
  13.4 0.2 copy-done.2
  13.6 0.3 multiply_reduce_fusion
  14.0 1.3 multiply_convert_fusion
  15.2 0.0 all-gather.6.cloned.1.call-update
  15.3 0.0 all-gather.4.cloned.1.call-start
  15.3 0.7 all-gather.4.cloned.1.call-update
  16.0 0.0 reduce-scatter.2.cloned.1.call-start
  16.1 0.2 multiply_reduce_fusion.2
  16.3 23.3 %all-gather = s32[16,1,1280]{2,1,0:T(1,128)S(1)} all-gather(s32[1,1,1280]{2,1,0:T(1,128)S(1)} %reshape.229), channel_id=1, replica_groups=mesh['genes'=16,'cols'=2] {'genes'}, dimensions={0}, use_global_device_ids=true | all-gather | bytes 87040 | tf_op jit(solution)/shard_map/all_gather | solution.py:74
  39.6 10.2 %all-gather.6.cloned.1.call-done = bf16[384,2560]{1,0:T(8,128)(2,1)} async-done(((bf16[384,1280]{1,0:T(8,128)(2,1)}), bf16[384,2560]{1,0:T(8,128)(2,1)}) %all-gather.6.cloned.1.call-update) | async-done | bytes 1966096 | tf_op jit(solution)/shard_map/all_gather | solution.py:73
  49.8 122.7 %all-gather.4.cloned.1.call-done = bf16[384,20480]{1,0:T(8,128)(2,1)} async-done(((bf16[384,1280]{1,0:T(8,128)(2,1)}), bf16[384,20480]{1,0:T(8,128)(2,1)}) %all-gather.4.cloned.1.call-update) | async-done | bytes 15728656 | tf_op jit(solution)/shard_map/all_gather | solution.py:79
  172.5 124.2 %while.14 = (s32[]{:T(128)}, f32[2560,300]{0,1:T(8,128)}, bf16[384,20480]{1,0:T(8,128)(2,1)}, bf16[384,2560]{1,0:T(8,128)(2,1)}, s32[20480]{0:T(1024)S(1)}, /*index=5*/s32[]{:T(128)}, s32[]{:T(128)}, s32[]{:T(128)}, s32[]{:T(128)}) while((s32[]{:T(128)}, f32[2560,300]{0,1:T(8,128)}, bf16[384,20480]{1,0:T(8,128)(2,1)}, ...), condition=%wide.region_4.5_spmd.clone, body=%wide.region_3.4_spmd.clone.sunk | while | flops 35970764800 | bytes 120955040 | solution.py:65
  172.5 37.4 %fusion.clone.9 = bf16[2560,10240]{0,1:T(8,128)(2,1)} fusion(bf16[384,2560]{1,0:T(8,128)(2,1)} %get-tuple-element.184, bf16[384,20480]{1,0:T(8,128)(2,1)} %get-tuple-element.183, s32[]{:T(128)S(6)} %select_n.27), kind=kOutput, calls=%fused_computation.2.clone.clone.clone.clone.clone.2.clone.1 | convolution fusion | flops 20237516800 | bytes 62259204 | tf_op jit(solution)/shard_map/while/body/eval_jaxpr/dot_general | solution.py:44
  209.9 24.2 %fusion.47 = f32[2560,300]{0,1:T(8,128)} fusion(s32[10240]{0:T(1024)S(1)} %dynamic_slice.28, f32[2560,300]{0,1:T(8,128)} %get-tuple-element.173, pred[]{:T(512)S(6)} %compare.3, bf16[2560,10240]{0,1:T(8,128)(2,1)} %fusion.clone.9), kind=kOutput, calls=%fused_computation.7.clone.3 | convolution fusion | flops 15733248000 | bytes 58613760 | tf_op jit(solution)/shard_map/while/body/eval_jaxpr/dot_general | solution.py:52
  234.1 37.4 %fusion.clone.9 = bf16[2560,10240]{0,1:T(8,128)(2,1)} fusion(bf16[384,2560]{1,0:T(8,128)(2,1)} %get-tuple-element.184, bf16[384,20480]{1,0:T(8,128)(2,1)} %get-tuple-element.183, s32[]{:T(128)S(6)} %select_n.27), kind=kOutput, calls=%fused_computation.2.clone.clone.clone.clone.clone.2.clone.1 | convolution fusion | flops 20237516800 | bytes 62259204 | tf_op jit(solution)/shard_map/while/body/eval_jaxpr/dot_general | solution.py:44
  271.6 25.1 %fusion.47 = f32[2560,300]{0,1:T(8,128)} fusion(s32[10240]{0:T(1024)S(1)} %dynamic_slice.28, f32[2560,300]{0,1:T(8,128)} %get-tuple-element.173, pred[]{:T(512)S(6)} %compare.3, bf16[2560,10240]{0,1:T(8,128)(2,1)} %fusion.clone.9), kind=kOutput, calls=%fused_computation.7.clone.3 | convolution fusion | flops 15733248000 | bytes 58613760 | tf_op jit(solution)/shard_map/while/body/eval_jaxpr/dot_general | solution.py:52
  296.7 0.0 reduce-scatter.2.cloned.1.call-update
  296.7 0.7 copy-done.5
  297.4 40.6 %reduce-scatter.2.cloned.1.call-done = f32[1280,300]{0,1:T(8,128)} async-done(((f32[2560,300]{0,1:T(8,128)}), f32[1280,300]{0,1:T(8,128)}) %reduce-scatter.2.cloned.1.call-update) | async-done | bytes 1536016 | tf_op jit(solution)/shard_map/reduce_scatter | solution.py:84
  338.0 1.6 fusion.26
  339.7 0.6 stack.27
  340.3 0.6 stack.28
  340.9 0.6 stack_broadcast_in_dim.3
  341.5 1.4 stack.29
  342.9 2.1 fusion.12
  345.0 39.5 %psum.7 = f32[300,7]{0,1:T(8,128)S(1)} all-reduce(f32[300,7]{0,1:T(8,128)S(1)} %fusion.12), channel_id=1, replica_groups=mesh['genes'=16,'cols'=2] {'genes','cols'}, use_global_device_ids=true, to_apply=%region_8.9 | all-reduce | flops 2100 | bytes 16800 | tf_op jit(solution)/shard_map/psum | solution.py:85
  384.6 0.6 pad_maximum_fusion
  (24 shorter events, 0.1 us)
Async XLA Ops:
  7.2 1.6 copy-start
  7.2 42.6 %all-gather.6.cloned.1.call-start = ((), (), s32[]{:S(2)}) async-start(), calls=%async_computation.2 | async-start | bytes 2949120 | tf_op jit(solution)/shard_map/all_gather | solution.py:73
  11.5 2.1 copy-start.2
  14.0 2.1 copy-start.3
  15.3 157.2 %all-gather.4.cloned.1.call-start = ((), (), s32[]{:S(2)}) async-start(), calls=%async_computation.1 | async-start | bytes 16711680 | tf_op jit(solution)/shard_map/all_gather | solution.py:79
  16.0 322.0 %reduce-scatter.2.cloned.1.call-start = ((), (), s32[]{:S(2)}) async-start(), calls=%async_computation.3 | async-start | bytes 4669440 | tf_op jit(solution)/shard_map/reduce_scatter | solution.py:84
  296.7 0.7 copy-start.5
  296.7 41.4 %copy-start.4 = (s32[1280,300]{0,1:T(8,128)S(1)}, s32[1280,300]{0,1:T(8,128)}, u32[]{:S(2)}) copy-start(s32[1280,300]{0,1:T(8,128)} %param.8) | copy-start | bytes 4608004
  297.4 87.8 %copy-start.1 = (f32[384,1280]{1,0:T(8,128)S(1)}, f32[384,1280]{1,0:T(8,128)}, u32[]{:S(2)}) copy-start(f32[384,1280]{1,0:T(8,128)} %param.6) | copy-start | bytes 5898244
Sparse Core Ops, SparseCore 0:
  15.4 34.3 all-gather.5
  52.6 119.7 all-gather.3
  296.8 41.1 reduce-scatter.1
where the time goes:
time: 392 us
  waiting for transfers between devices  174 us (44%)
  matrix products  126 us (32%)
  blocking collectives  62.8 us (16%)
  between operations  13.9 us (4%)
  other arithmetic  7.47 us (2%)
  local copies, waits for them, and re-layouts  6.83 us (2%)
    all_gather x1, waiting for transfers between devices, local(): lax.all_gather(scaled, 'genes', axis=1, tiled=True)  123 us
    dot_general x2, matrix products, tile_term(): lax.dot_general(row_block, column_block, (((0,), (0,)), ((), ())), prefer...  74.9 us
    dot_general x2, matrix products, tile_term(): return jnp.dot(adjacency, member_block, preferred_element_type=jnp.float32)  49.3 us
    reduce_scatter x1, waiting for transfers between devices, local(): lax.psum_scatter(partial_value, 'cols', scatter_dimension=0, tiled=True)  40.6 us
    psum x1, blocking collectives, local(): lax.psum(local_sums(connectivity, labels, ref_kim), ('genes', 'cols'))  39.5 us
    all_gather x1, blocking collectives, local(): panel_ids = lax.all_gather(module_ids, 'genes', axis=0, tiled=True)  23.3 us
    all_gather x1, waiting for transfers between devices, local(): row_block = lax.all_gather(scaled, 'cols', axis=1, tiled=True)  10.2 us
  transfers between devices with their start and end apart: 3, of which 3 were waited for; matrix products, arithmetic and copies ran while one was open for 0% of the time, Pallas kernels for 0%

commit v1 on v0

--- a/solution.py
+++ b/solution.py
@@ -82,7 +82,9 @@
         module_count,
     )
     connectivity = lax.psum_scatter(partial_value, "cols", scatter_dimension=0, tiled=True)
-    sums = lax.psum(local_sums(connectivity, labels, ref_kim), ("genes", "cols"))
+    sums = jax.lax.psum(
+        jax.lax.psum(local_sums(connectivity, labels, ref_kim), axis_name="genes"), axis_name="cols"
+    )
     return (connectivity, preserve(sums, G))
 
 

time: 392 us -> 421 us (1.074)
  blocking collectives: 62.8 us -> 91.5 us
    psum x1 -> x2, blocking collectives: 39.5 us -> 68.2 us  [the longest x1 61.1 us: local(): jax.lax.psum(local_sums(connectivity, labels, ref_kim), axis_name='genes')]
where the time goes in v1:
time: 421 us; the launch traced here: 420 us
  waiting for transfers between devices  174 us (41%)
  matrix products  126 us (30%)
  blocking collectives  91.5 us (22%)
  between operations  13.9 us (3%)
  other arithmetic  7.47 us (2%)
  local copies, waits for them, and re-layouts  6.83 us (2%)
    all_gather x1, waiting for transfers between devices, local(): lax.all_gather(scaled, 'genes', axis=1, tiled=True)  123 us
    dot_general x2, matrix products, tile_term(): lax.dot_general(row_block, column_block, (((0,), (0,)), ((), ())), prefer...  74.9 us
    psum x1, blocking collectives, local(): jax.lax.psum(local_sums(connectivity, labels, ref_kim), axis_name='genes')  61.1 us
    dot_general x2, matrix products, tile_term(): return jnp.dot(adjacency, member_block, preferred_element_type=jnp.float32)  49.3 us
    reduce_scatter x1, waiting for transfers between devices, local(): lax.psum_scatter(partial_value, 'cols', scatter_dimension=0, tiled=True)  40.7 us
    all_gather x1, blocking collectives, local(): panel_ids = lax.all_gather(module_ids, 'genes', axis=0, tiled=True)  23.3 us
    all_gather x1, waiting for transfers between devices, local(): row_block = lax.all_gather(scaled, 'cols', axis=1, tiled=True)  10.2 us
  transfers between devices with their start and end apart: 3, of which 3 were waited for; matrix products, arithmetic and copies ran while one was open for 0% of the time, Pallas kernels for 0%

profile of v1, /device:TPU:0, one launch (start us, length us, event | category | flops | bytes accessed | tf_op | source)
XLA Modules:
  0.0 420.4 jit_solution(6319321116603394755)
XLA Ops:
  7.2 0.0 all-gather.6.cloned.1.call-start
  7.2 0.8 compare_select_fusion
  8.0 0.7 compare_and_fusion
  8.8 2.7 gather_fusion
  11.5 1.9 select_reduce_fusion
  13.4 0.2 copy-done.2
  13.6 0.3 multiply_reduce_fusion
  14.0 1.3 multiply_convert_fusion
  15.2 0.0 all-gather.6.cloned.1.call-update
  15.3 0.0 all-gather.4.cloned.1.call-start
  15.3 0.7 all-gather.4.cloned.1.call-update
  16.0 0.0 reduce-scatter.2.cloned.1.call-start
  16.1 0.2 multiply_reduce_fusion.2
  16.3 23.3 %all-gather = s32[16,1,1280]{2,1,0:T(1,128)S(1)} all-gather(s32[1,1,1280]{2,1,0:T(1,128)S(1)} %reshape.229), channel_id=1, replica_groups=mesh['genes'=16,'cols'=2] {'genes'}, dimensions={0}, use_global_device_ids=true | all-gather | bytes 87040 | tf_op jit(solution)/shard_map/all_gather | solution.py:74
  39.6 10.2 %all-gather.6.cloned.1.call-done = bf16[384,2560]{1,0:T(8,128)(2,1)} async-done(((bf16[384,1280]{1,0:T(8,128)(2,1)}), bf16[384,2560]{1,0:T(8,128)(2,1)}) %all-gather.6.cloned.1.call-update) | async-done | bytes 1966096 | tf_op jit(solution)/shard_map/all_gather | solution.py:73
  49.8 122.7 %all-gather.4.cloned.1.call-done = bf16[384,20480]{1,0:T(8,128)(2,1)} async-done(((bf16[384,1280]{1,0:T(8,128)(2,1)}), bf16[384,20480]{1,0:T(8,128)(2,1)}) %all-gather.4.cloned.1.call-update) | async-done | bytes 15728656 | tf_op jit(solution)/shard_map/all_gather | solution.py:79
  172.5 124.2 %while.14 = (s32[]{:T(128)}, f32[2560,300]{0,1:T(8,128)}, bf16[384,20480]{1,0:T(8,128)(2,1)}, bf16[384,2560]{1,0:T(8,128)(2,1)}, s32[20480]{0:T(1024)S(1)}, /*index=5*/s32[]{:T(128)}, s32[]{:T(128)}, s32[]{:T(128)}, s32[]{:T(128)}) while((s32[]{:T(128)}, f32[2560,300]{0,1:T(8,128)}, bf16[384,20480]{1,0:T(8,128)(2,1)}, ...), condition=%wide.region_4.5_spmd.clone, body=%wide.region_3.4_spmd.clone.sunk | while | flops 35970764800 | bytes 120955040 | solution.py:65
  172.5 37.4 %fusion.clone.9 = bf16[2560,10240]{0,1:T(8,128)(2,1)} fusion(bf16[384,2560]{1,0:T(8,128)(2,1)} %get-tuple-element.184, bf16[384,20480]{1,0:T(8,128)(2,1)} %get-tuple-element.183, s32[]{:T(128)S(6)} %select_n.27), kind=kOutput, calls=%fused_computation.2.clone.clone.clone.clone.clone.2.clone.1 | convolution fusion | flops 20237516800 | bytes 62259204 | tf_op jit(solution)/shard_map/while/body/eval_jaxpr/dot_general | solution.py:44
  209.9 24.2 %fusion.47 = f32[2560,300]{0,1:T(8,128)} fusion(s32[10240]{0:T(1024)S(1)} %dynamic_slice.28, f32[2560,300]{0,1:T(8,128)} %get-tuple-element.173, pred[]{:T(512)S(6)} %compare.3, bf16[2560,10240]{0,1:T(8,128)(2,1)} %fusion.clone.9), kind=kOutput, calls=%fused_computation.7.clone.3 | convolution fusion | flops 15733248000 | bytes 58613760 | tf_op jit(solution)/shard_map/while/body/eval_jaxpr/dot_general | solution.py:52
  234.1 37.4 %fusion.clone.9 = bf16[2560,10240]{0,1:T(8,128)(2,1)} fusion(bf16[384,2560]{1,0:T(8,128)(2,1)} %get-tuple-element.184, bf16[384,20480]{1,0:T(8,128)(2,1)} %get-tuple-element.183, s32[]{:T(128)S(6)} %select_n.27), kind=kOutput, calls=%fused_computation.2.clone.clone.clone.clone.clone.2.clone.1 | convolution fusion | flops 20237516800 | bytes 62259204 | tf_op jit(solution)/shard_map/while/body/eval_jaxpr/dot_general | solution.py:44
  271.6 25.1 %fusion.47 = f32[2560,300]{0,1:T(8,128)} fusion(s32[10240]{0:T(1024)S(1)} %dynamic_slice.28, f32[2560,300]{0,1:T(8,128)} %get-tuple-element.173, pred[]{:T(512)S(6)} %compare.3, bf16[2560,10240]{0,1:T(8,128)(2,1)} %fusion.clone.9), kind=kOutput, calls=%fused_computation.7.clone.3 | convolution fusion | flops 15733248000 | bytes 58613760 | tf_op jit(solution)/shard_map/while/body/eval_jaxpr/dot_general | solution.py:52
  296.7 0.7 copy-done.5
  297.4 40.7 %reduce-scatter.2.cloned.1.call-done = f32[1280,300]{0,1:T(8,128)} async-done(((f32[2560,300]{0,1:T(8,128)}), f32[1280,300]{0,1:T(8,128)}) %reduce-scatter.2.cloned.1.call-update) | async-done | bytes 1536016 | tf_op jit(solution)/shard_map/reduce_scatter | solution.py:84
  338.1 1.6 fusion.26
  339.8 0.6 stack.27
  340.4 0.6 stack.28
  340.9 0.6 stack_broadcast_in_dim.3
  341.5 1.4 stack.29
  342.9 2.1 fusion.12
  345.0 61.1 %psum.14 = f32[300,7]{0,1:T(8,128)S(1)} all-reduce(f32[300,7]{0,1:T(8,128)S(1)} %fusion.12), channel_id=1, replica_groups=mesh['genes'=16,'cols'=2] {'genes'}, use_global_device_ids=true, to_apply=%region_8.9 | all-reduce | flops 2100 | bytes 16800 | tf_op jit(solution)/shard_map/psum | solution.py:86
  406.1 7.1 %psum.15 = f32[300,7]{0,1:T(8,128)S(1)} all-reduce(f32[300,7]{0,1:T(8,128)S(1)} %psum.14), channel_id=1, replica_groups=mesh['genes'=16,'cols'=2] {'cols'}, use_global_device_ids=true, to_apply=%region_9.10 | all-reduce | flops 2100 | bytes 16800 | tf_op jit(solution)/shard_map/psum | solution.py:85
  413.3 0.6 pad_maximum_fusion
  (25 shorter events, 0.2 us)
Async XLA Ops:
  7.2 1.6 copy-start
  7.2 42.6 %all-gather.6.cloned.1.call-start = ((), (), s32[]{:S(2)}) async-start(), calls=%async_computation.2 | async-start | bytes 2949120 | tf_op jit(solution)/shard_map/all_gather | solution.py:73
  11.5 2.1 copy-start.2
  14.0 2.1 copy-start.3
  15.3 157.2 %all-gather.4.cloned.1.call-start = ((), (), s32[]{:S(2)}) async-start(), calls=%async_computation.1 | async-start | bytes 16711680 | tf_op jit(solution)/shard_map/all_gather | solution.py:79
  16.0 322.1 %reduce-scatter.2.cloned.1.call-start = ((), (), s32[]{:S(2)}) async-start(), calls=%async_computation.3 | async-start | bytes 4669440 | tf_op jit(solution)/shard_map/reduce_scatter | solution.py:84
  296.7 0.7 copy-start.5
  296.7 41.4 %copy-start.4 = (s32[1280,300]{0,1:T(8,128)S(1)}, s32[1280,300]{0,1:T(8,128)}, u32[]{:S(2)}) copy-start(s32[1280,300]{0,1:T(8,128)} %param.8) | copy-start | bytes 4608004
  297.4 116.5 %copy-start.1 = (f32[384,1280]{1,0:T(8,128)S(1)}, f32[384,1280]{1,0:T(8,128)}, u32[]{:S(2)}) copy-start(f32[384,1280]{1,0:T(8,128)} %param.6) | copy-start | bytes 5898244
Sparse Core Ops, SparseCore 0:
  15.4 34.3 all-gather.5
  52.6 119.7 all-gather.3
  296.8 41.1 reduce-scatter.1
